TPU v7x, 32 devices: a whole 2x2x4 slice. The times are simulated.
32 devices in a mesh: seq: 2 (over x), head: 4 (over z), dp: 4 (over y, core).
Axes of the slice: x: 2, y: 2, z: 4, core: 2. Of those that a mesh axis runs over, the one named last changes fastest.
Arguments:
- queries: bfloat16 [4, 512, 64, 128], P('dp', 'seq', 'head'), may hold values from -6 to 6
- keys: bfloat16 [4, 512, 8, 128], P('dp', 'seq', 'head'), may hold values from -6 to 6
- values: bfloat16 [4, 512, 8, 128], P('dp', 'seq', 'head'), may hold values from -6 to 6
- attn_out: bfloat16 [4, 512, 64, 128], P('dp', 'seq', 'head'), may hold values from -6 to 6
- out_grad: bfloat16 [4, 512, 64, 128], P('dp', 'seq', 'head'), may hold values from -6 to 6
- gate_values: float32 [4, 64, 512], P('dp', 'head', 'seq'), may hold values from 0.05 to 0.95
- log_totals: float32 [4, 64, 512], P('dp', 'head', 'seq'), may hold values from 3 to 5
- hidden: bfloat16 [4, 512, 5120], P('dp', 'seq', 'head'), may hold values from -6 to 6
- block_ids: int32 [4, 8, 8, 16], P('dp', 'seq', 'head'), may hold values from 0 to 7, as said below
- block_valid: int32 [4, 8, 8, 16], P('dp', 'seq', 'head'), may hold values from 0 to 1
Outputs:
- query_grad: bfloat16 [4, 512, 64, 128], P('dp', 'seq', 'head')
- key_grad: bfloat16 [4, 512, 8, 128], P('dp', 'seq', 'head')
- value_grad: bfloat16 [4, 512, 8, 128], P('dp', 'seq', 'head')
- gate_weight_grad: float32 [64, 5120], P(None, 'head')
Inputs may be any that keep to these rules, and one draw needn't show every extreme that they name: `block_ids`: for query tile t and key head k, the slots whose block_valid is 1 name distinct blocks of index at most t, among them block t itself and block 0; exactly min(16, t + 1) slots are valid. The ids of the other slots are any blocks, and may repeat a valid one.
All inputs are finite; a program needn't handle non-finite values.
Results may differ from a plain program's by a relative error of at most 0.025.
Values may be sent and summed in bfloat16 or wider, within the bound.
A program may use at most 128 MiB of HBM per device.

v0:
```python
import math
import jax
import jax.numpy as jnp
from jax import lax
from jax.sharding import PartitionSpec as P


def on_device(
    queries,
    keys,
    values,
    attn_out,
    out_grad,
    gate_values,
    log_totals,
    hidden,
    block_ids,
    block_valid,
):
    tokens_here = queries.shape[1]
    heads_here = queries.shape[2]
    kv_heads = keys.shape[2]
    head_width = queries.shape[3]
    group_size = heads_here // kv_heads
    tiles_here = block_ids.shape[1]
    block_rows = tokens_here // tiles_here
    seq_count = lax.axis_size("seq")
    all_blocks = tiles_here * seq_count
    factor = head_width ** (-0.5)
    chosen = block_ids[0]
    usable = block_valid[0] > 0
    head_rows = jnp.arange(kv_heads, dtype=jnp.int32)[None, :, None]
    offsets = jnp.arange(block_rows, dtype=jnp.int32)
    whole_keys, whole_values = (
        lax.all_gather(keys, "seq", axis=1, tiled=True),
        lax.all_gather(values, "seq", axis=1, tiled=True),
    )
    key_sel = whole_keys[0].reshape(all_blocks, block_rows, kv_heads, head_width)[
        chosen, :, head_rows, :
    ]
    value_sel = whole_values[0].reshape(all_blocks, block_rows, kv_heads, head_width)[
        chosen, :, head_rows, :
    ]
    query_tiles = queries[0].reshape(tiles_here, block_rows, kv_heads, group_size, head_width)
    output_tiles = attn_out[0].reshape(tiles_here, block_rows, kv_heads, group_size, head_width)
    upstream_tiles = out_grad[0].reshape(tiles_here, block_rows, kv_heads, group_size, head_width)
    gate_tiles = jnp.transpose(
        gate_values[0].reshape(kv_heads, group_size, tiles_here, block_rows), (2, 0, 1, 3)
    )
    total_tiles = jnp.transpose(
        log_totals[0].reshape(kv_heads, group_size, tiles_here, block_rows), (2, 0, 1, 3)
    )
    tile_numbers = lax.axis_index("seq") * tiles_here + jnp.arange(tiles_here, dtype=jnp.int32)

    def tile_math(tile_items):
        (
            tile_number,
            query_tile,
            output_tile,
            upstream,
            gate_tile,
            totals,
            picked,
            usable_tile,
            key_tile,
            value_tile,
        ) = tile_items
        gates_by_row = jnp.transpose(gate_tile, (2, 0, 1))
        grad_output = (gates_by_row[..., None] * upstream.astype(jnp.float32)).astype(jnp.bfloat16)
        output_wide = output_tile.astype(jnp.float32)
        row_delta = jnp.transpose(
            jnp.sum(grad_output.astype(jnp.float32) * output_wide, axis=-1), (1, 2, 0)
        )
        gate_grad = jnp.sum(upstream.astype(jnp.float32) * output_wide, axis=-1)
        logit_grad = (gate_grad * gates_by_row * (1.0 - gates_by_row)).astype(jnp.bfloat16)
        scores = (
            jnp.einsum("ikgd,knjd->kginj", query_tile, key_tile, preferred_element_type=jnp.float32)
            * factor
        )
        query_pos = tile_number * block_rows + offsets
        key_pos = picked[..., None] * block_rows + offsets
        allowed = usable_tile[:, None, :, None] & (
            key_pos[:, None, :, :] <= query_pos[None, :, None, None]
        )
        probability = jnp.where(allowed[:, None], jnp.exp(scores - totals[..., None, None]), 0.0)
        prob_grad = jnp.einsum(
            "ikgd,knjd->kginj", grad_output, value_tile, preferred_element_type=jnp.float32
        )
        dscore = (probability * (prob_grad - row_delta[..., None, None])).astype(jnp.bfloat16)
        prob_low = probability.astype(jnp.bfloat16)
        query_part = (
            jnp.einsum("kginj,knjd->ikgd", dscore, key_tile, preferred_element_type=jnp.float32)
            * factor
        ).astype(jnp.bfloat16)
        key_part = (
            jnp.einsum("kginj,ikgd->knjd", dscore, query_tile, preferred_element_type=jnp.float32)
            * factor
        )
        value_part = jnp.einsum(
            "kginj,ikgd->knjd", prob_low, grad_output, preferred_element_type=jnp.float32
        )
        return (query_part, logit_grad, jnp.concatenate([key_part, value_part], axis=-1))

    def tile_step(partial_value, tile_items):
        query_part, logit_grad, paired = tile_math(tile_items)
        return (partial_value, (query_part, logit_grad, paired))

    tile_items = (
        tile_numbers,
        query_tiles,
        output_tiles,
        upstream_tiles,
        gate_tiles,
        total_tiles,
        chosen,
        usable,
        key_sel,
        value_sel,
    )
    unused, (query_parts, logit_parts, paired_all) = lax.scan(
        tile_step, jnp.zeros((), jnp.float32), tile_items
    )
    span_blocks = tokens_here * lax.axis_size("seq") // block_rows
    target = chosen
    target = jnp.where((target >= 0) & (target < span_blocks), target, span_blocks)
    holder = jnp.zeros((span_blocks, block_rows, kv_heads, 2 * head_width), jnp.float32)
    holder = holder.at[target, :, head_rows, :].add(paired_all, mode="drop")
    summed = lax.psum_scatter(
        holder.reshape(tokens_here * lax.axis_size("seq"), kv_heads, 2 * head_width).astype(
            jnp.bfloat16
        ),
        "seq",
        scatter_dimension=0,
        tiled=True,
    ).astype(jnp.float32)
    query_grad = query_parts.reshape(1, tokens_here, heads_here, head_width)
    logit_rows = jnp.transpose(logit_parts.reshape(tokens_here, heads_here))[None]
    every_logit = lax.all_gather(logit_rows, "head", axis=1, tiled=True)
    weight_part = jnp.dot(every_logit[0], hidden[0], preferred_element_type=jnp.float32)
    weight_scale = 1.0 / math.sqrt(lax.axis_size("dp") * seq_count * tokens_here)
    gate_weight_grad = lax.psum(weight_part, ("seq", "dp")) * weight_scale
    key_grad = summed[None, :, :, :head_width].astype(jnp.bfloat16)
    value_grad = summed[None, :, :, head_width:].astype(jnp.bfloat16)
    return (query_grad, key_grad, value_grad, gate_weight_grad)


def solution(mesh):
    return jax.shard_map(
        on_device,
        mesh=mesh,
        in_specs=(
            P("dp", "seq", "head", None),
            P("dp", "seq", "head", None),
            P("dp", "seq", "head", None),
            P("dp", "seq", "head", None),
            P("dp", "seq", "head", None),
            P("dp", "head", "seq"),
            P("dp", "head", "seq"),
            P("dp", "seq", "head"),
            P("dp", "seq", "head", None),
            P("dp", "seq", "head", None),
        ),
        out_specs=(
            P("dp", "seq", "head", None),
            P("dp", "seq", "head", None),
            P("dp", "seq", "head", None),
            P(None, "head"),
        ),
        check_vma=False,
    )
```

profile of v0, /device:TPU:0, one launch (start us, length us, event | category | flops | bytes accessed | tf_op | source)
XLA Modules:
  0.0 180.2 jit_solution(4722716227157090044)
XLA Ops:
  9.0 7.1 %all_gather.9 = bf16[1,512,2,128]{3,1,2,0:T(8,128)(2,1)S(1)} all-gather(bf16[1,256,2,128]{3,1,2,0:T(8,128)(2,1)S(1)} %copy.32), channel_id=1, replica_groups=mesh['seq'=2,'head'=4,'dp'=4] {'seq'}, dimensions={1}, use_global_device_ids=true | all-gather | bytes 393216 | tf_op jit(solution)/shard_map/all_gather | solution.py:35
  19.4 5.6 %all_gather.10 = bf16[1,512,2,128]{3,1,2,0:T(8,128)(2,1)S(1)} all-gather(bf16[1,256,2,128]{3,1,2,0:T(8,128)(2,1)S(1)} %copy.35), channel_id=1, replica_groups=mesh['seq'=2,'head'=4,'dp'=4] {'seq'}, dimensions={1}, use_global_device_ids=true | all-gather | bytes 393216 | tf_op jit(solution)/shard_map/all_gather | solution.py:36
  25.1 1.1 gather_fusion
  26.1 2.3 %gather_fusion.1 = bf16[128,64,128]{2,1,0:T(8,128)(2,1)} fusion(bf16[8,64,2,128]{3,1,2,0:T(8,128)(2,1)S(1)} %copy.36, s32[128]{0:T(128)S(1)} %reshape.124), kind=kCustom, calls=%fused_computation.1 | custom fusion | bytes 4195328 | tf_op jit(solution)/shard_map/gather | solution.py:41
  28.6 69.9 %while.16 = (s32[]{:T(128)}, bf16[4,64,2,8,128]{4,3,2,1,0:T(8,128)(2,1)}, bf16[4,64,2,8]{1,3,2,0:T(8,128)(2,1)S(1)}, f32[4,2,16,64,256]{4,3,2,1,0:T(8,128)}, bf1...) while((s32[]{:T(128)}, ...), condition=%wide.region_3.4_spmd.clone.clone, body=%wide.region_0.3_spmd.clone.clone.sunk | while | flops 1355944064 | bytes 33248452 | solution.py:120
  29.6 1.3 fusion.78
  30.8 1.1 constant_dynamic-slice_fusion.11
  35.0 4.0 %fusion.82 = bf16[2,8,64,16,64]{2,4,1,3,0:T(8,128)(2,1)S(1)} fusion(f32[2,16,64,64,8]{3,2,4,1,0:T(8,128)S(1)} %fusion.78, f32[2,8,64]{2,1,0:T(8,128)S(1)} %bitcast.222, f32[2,8,64]{2,1,0:T(8,128)S(1)} %bitcast.223, pred[2,64,16,64]{1,3,2,0:T(8,128)(4,1)S(1)} %compare_and_fusion.2, bf16[4,2,16,64,128]{4,3,2,1,0:T(8,128)(2,1)} %get-tuple-element.380, ...), kind=kOutput, calls=%fused_computation.6.clone.1 | convolution fusion | flops 275120128 | bytes 7221252 | tf_op jit(solution)/shard_map/while/body/eval_jaxpr/ikgd,knjd->kginj/dot_general | solution.py:86
  39.0 1.3 fusion.83
  41.2 2.4 %fusion.85 = f32[2,16,64,128]{3,2,1,0:T(8,128)S(1)} fusion(f32[2,16,64,64,8]{3,2,4,1,0:T(8,128)S(1)} %fusion.78, f32[2,8,64]{2,1,0:T(8,128)S(1)} %bitcast.224, pred[2,64,16,64]{1,3,2,0:T(8,128)(4,1)S(1)} %compare_and_fusion.2, f32[64,2,8]{0,2,1:T(8,128)S(1)} %bitcast.216, bf16[1,64,2,8,128]{4,3,2,1,0:T(8,128)(2,1)S(1)} %get-tuple-element.332), kind=kOutput, calls=%fused_computation.17.clone.1 | convolution fusion | flops 273022976 | bytes 5644288 | tf_op jit(solution)/shard_map/while/body/eval_jaxpr/kginj,ikgd->knjd/dot_general | solution.py:99
  44.6 1.5 fusion.87
  47.0 1.3 fusion.78
  48.3 1.1 constant_dynamic-slice_fusion.11
  52.4 4.0 %fusion.82 = bf16[2,8,64,16,64]{2,4,1,3,0:T(8,128)(2,1)S(1)} fusion(f32[2,16,64,64,8]{3,2,4,1,0:T(8,128)S(1)} %fusion.78, f32[2,8,64]{2,1,0:T(8,128)S(1)} %bitcast.222, f32[2,8,64]{2,1,0:T(8,128)S(1)} %bitcast.223, pred[2,64,16,64]{1,3,2,0:T(8,128)(4,1)S(1)} %compare_and_fusion.2, bf16[4,2,16,64,128]{4,3,2,1,0:T(8,128)(2,1)} %get-tuple-element.380, ...), kind=kOutput, calls=%fused_computation.6.clone.1 | convolution fusion | flops 275120128 | bytes 7221252 | tf_op jit(solution)/shard_map/while/body/eval_jaxpr/ikgd,knjd->kginj/dot_general | solution.py:86
  56.5 1.3 fusion.83
  58.7 2.4 %fusion.85 = f32[2,16,64,128]{3,2,1,0:T(8,128)S(1)} fusion(f32[2,16,64,64,8]{3,2,4,1,0:T(8,128)S(1)} %fusion.78, f32[2,8,64]{2,1,0:T(8,128)S(1)} %bitcast.224, pred[2,64,16,64]{1,3,2,0:T(8,128)(4,1)S(1)} %compare_and_fusion.2, f32[64,2,8]{0,2,1:T(8,128)S(1)} %bitcast.216, bf16[1,64,2,8,128]{4,3,2,1,0:T(8,128)(2,1)S(1)} %get-tuple-element.332), kind=kOutput, calls=%fused_computation.17.clone.1 | convolution fusion | flops 273022976 | bytes 5644288 | tf_op jit(solution)/shard_map/while/body/eval_jaxpr/kginj,ikgd->knjd/dot_general | solution.py:99
  62.1 1.4 fusion.87
  64.5 1.3 fusion.78
  65.7 1.1 constant_dynamic-slice_fusion.11
  69.9 4.0 %fusion.82 = bf16[2,8,64,16,64]{2,4,1,3,0:T(8,128)(2,1)S(1)} fusion(f32[2,16,64,64,8]{3,2,4,1,0:T(8,128)S(1)} %fusion.78, f32[2,8,64]{2,1,0:T(8,128)S(1)} %bitcast.222, f32[2,8,64]{2,1,0:T(8,128)S(1)} %bitcast.223, pred[2,64,16,64]{1,3,2,0:T(8,128)(4,1)S(1)} %compare_and_fusion.2, bf16[4,2,16,64,128]{4,3,2,1,0:T(8,128)(2,1)} %get-tuple-element.380, ...), kind=kOutput, calls=%fused_computation.6.clone.1 | convolution fusion | flops 275120128 | bytes 7221252 | tf_op jit(solution)/shard_map/while/body/eval_jaxpr/ikgd,knjd->kginj/dot_general | solution.py:86
  73.9 1.3 fusion.83
  76.1 2.4 %fusion.85 = f32[2,16,64,128]{3,2,1,0:T(8,128)S(1)} fusion(f32[2,16,64,64,8]{3,2,4,1,0:T(8,128)S(1)} %fusion.78, f32[2,8,64]{2,1,0:T(8,128)S(1)} %bitcast.224, pred[2,64,16,64]{1,3,2,0:T(8,128)(4,1)S(1)} %compare_and_fusion.2, f32[64,2,8]{0,2,1:T(8,128)S(1)} %bitcast.216, bf16[1,64,2,8,128]{4,3,2,1,0:T(8,128)(2,1)S(1)} %get-tuple-element.332), kind=kOutput, calls=%fused_computation.17.clone.1 | convolution fusion | flops 273022976 | bytes 5644288 | tf_op jit(solution)/shard_map/while/body/eval_jaxpr/kginj,ikgd->knjd/dot_general | solution.py:99
  79.5 1.5 fusion.87
  81.9 1.3 fusion.78
  87.3 4.0 %fusion.82 = bf16[2,8,64,16,64]{2,4,1,3,0:T(8,128)(2,1)S(1)} fusion(f32[2,16,64,64,8]{3,2,4,1,0:T(8,128)S(1)} %fusion.78, f32[2,8,64]{2,1,0:T(8,128)S(1)} %bitcast.222, f32[2,8,64]{2,1,0:T(8,128)S(1)} %bitcast.223, pred[2,64,16,64]{1,3,2,0:T(8,128)(4,1)S(1)} %compare_and_fusion.2, bf16[4,2,16,64,128]{4,3,2,1,0:T(8,128)(2,1)} %get-tuple-element.380, ...), kind=kOutput, calls=%fused_computation.6.clone.1 | convolution fusion | flops 275120128 | bytes 7221252 | tf_op jit(solution)/shard_map/while/body/eval_jaxpr/ikgd,knjd->kginj/dot_general | solution.py:86
  91.4 1.3 fusion.83
  93.6 2.4 %fusion.85 = f32[2,16,64,128]{3,2,1,0:T(8,128)S(1)} fusion(f32[2,16,64,64,8]{3,2,4,1,0:T(8,128)S(1)} %fusion.78, f32[2,8,64]{2,1,0:T(8,128)S(1)} %bitcast.224, pred[2,64,16,64]{1,3,2,0:T(8,128)(4,1)S(1)} %compare_and_fusion.2, f32[64,2,8]{0,2,1:T(8,128)S(1)} %bitcast.216, bf16[1,64,2,8,128]{4,3,2,1,0:T(8,128)(2,1)S(1)} %get-tuple-element.332), kind=kOutput, calls=%fused_computation.17.clone.1 | convolution fusion | flops 273022976 | bytes 5644288 | tf_op jit(solution)/shard_map/while/body/eval_jaxpr/kginj,ikgd->knjd/dot_general | solution.py:99
  96.9 1.5 fusion.87
  98.5 13.6 %all-gather = bf16[64,256]{1,0:T(8,128)(2,1)S(1)} all-gather(bf16[16,256]{1,0:T(8,128)(2,1)S(1)} %bitcast.227), channel_id=2, replica_groups=mesh['seq'=2,'head'=4,'dp'=4] {'head'}, dimensions={0}, use_global_device_ids=true | all-gather | bytes 40960 | tf_op jit(solution)/shard_map/all_gather | solution.py:138
  113.4 19.1 %scatter_fusion = f32[8,64,2,256]{3,1,2,0:T(8,128)S(1)} fusion(f32[8,64,2,256]{3,1,2,0:T(8,128)S(1)} %broadcast_in_dim.53, s32[128]{0:T(128)S(1)} %reshape.136, f32[128,64,256]{2,1,0:T(8,128)} %bitcast.210), kind=kCustom, calls=%fused_computation.2 | custom fusion | flops 2097152 | bytes 25166848 | tf_op jit(solution)/shard_map/scatter-add | solution.py:127
  133.4 35.1 %all-reduce.2.cloned.1.call-done = f32[64,1280]{1,0:T(8,128)} async-done(((f32[64,1280]{1,0:T(8,128)}), f32[64,1280]{1,0:T(8,128)}) %all-reduce.2.cloned.1.call-update) | async-done | bytes 327696 | tf_op jit(solution)/shard_map/psum | solution.py:141
  168.5 1.7 broadcast_multiply_fusion
  (81 shorter events, 30.9 us)
Async XLA Ops:
  8.0 104.2 %copy-start = (bf16[1,256,1280]{2,1,0:T(8,128)(2,1)S(1)}, bf16[1,256,1280]{2,1,0:T(8,128)(2,1)}, u32[]{:S(2)}) copy-start(bf16[1,256,1280]{2,1,0:T(8,128)(2,1)} %param.19) | copy-start | bytes 1966084
  8.0 20.5 %copy-start.1 = (f32[1,16,256]{2,1,0:T(8,128)S(1)}, f32[1,16,256]{2,1,0:T(8,128)}, u32[]{:S(2)}) copy-start(f32[1,16,256]{2,1,0:T(8,128)} %param.17) | copy-start | bytes 49156
  8.0 160.4 %all-reduce.2.cloned.1.call-start = ((), (), s32[]{:S(2)}) async-start(), calls=%async_computation.2 | async-start | bytes 655360 | tf_op jit(solution)/shard_map/psum | solution.py:141
  113.2 57.0 %reduce-scatter.2.cloned.1.call-start = ((), (), s32[]{:S(2)}) async-start(), calls=%async_computation.1 | async-start | bytes 786432 | tf_op jit(solution)/shard_map/reduce_scatter | solution.py:128
Sparse Core Ops, SparseCore 0:
  113.3 55.1 all-reduce.1
Sparse Core Ops, SparseCore 1:
  133.5 15.6 reduce-scatter.1
where the time goes:
time: 181 us; the launch traced here: 180 us
  matrix products  40.9 us (23%)
  other arithmetic  35.2 us (19%)
  waiting for transfers between devices  35.1 us (19%)
  blocking collectives  26.4 us (15%)
  local copies, waits for them, and re-layouts  24.1 us (13%)
  between operations  15.6 us (9%)
  loops' own time  2.88 us (2%)
    psum x1, waiting for transfers between devices, on_device(): gate_weight_grad = lax.psum(weight_part, ('seq', 'dp')) * weight_scale  35.1 us
    scatter-add x1, other arithmetic, on_device(): holder = holder.at[target, :, head_rows, :].add(paired_all, mode='drop')  19.1 us
    dot_general x4, matrix products, tile_math(): jnp.einsum('ikgd,knjd->kginj', grad_output, value_tile, preferred_element...  16.1 us
    all_gather x1, blocking collectives, on_device(): every_logit = lax.all_gather(logit_rows, 'head', axis=1, tiled=True)  13.6 us
    dynamic_slice x16, local copies, waits for them, and re-layouts, on_device(): lax.scan(tile_step, jnp.zeros((), jnp.float32), tile_items)  10.6 us
    dot_general x4, matrix products, tile_math(): jnp.einsum('kginj,ikgd->knjd', prob_low, grad_output, preferred_element_t...  9.55 us
    all_gather x1, blocking collectives, on_device(): lax.all_gather(keys, 'seq', axis=1, tiled=True)  7.12 us
    dynamic_update_slice x8, other arithmetic, on_device(): lax.scan(tile_step, jnp.zeros((), jnp.float32), tile_items)  5.93 us
  transfers between devices with their start and end apart: 2, of which 1 were waited for; matrix products, arithmetic and copies ran while one was open for 12% of the time, Pallas kernels for 0%

commit v1 on v0

--- a/solution.py
+++ b/solution.py
@@ -138,7 +138,7 @@
     every_logit = lax.all_gather(logit_rows, "head", axis=1, tiled=True)
     weight_part = jnp.dot(every_logit[0], hidden[0], preferred_element_type=jnp.float32)
     weight_scale = 1.0 / math.sqrt(lax.axis_size("dp") * seq_count * tokens_here)
-    gate_weight_grad = lax.psum(weight_part, ("seq", "dp")) * weight_scale
+    gate_weight_grad = lax.psum(lax.psum(weight_part, "dp"), "seq") * weight_scale
     key_grad = summed[None, :, :, :head_width].astype(jnp.bfloat16)
     value_grad = summed[None, :, :, head_width:].astype(jnp.bfloat16)
     return (query_grad, key_grad, value_grad, gate_weight_grad)

time: 181 us -> 200 us (1.10)
  waiting for transfers between devices: 35.1 us -> 55.3 us
    reduce_scatter x1, waiting for transfers between devices: 0.01 us -> 15.2 us  [on_device(): lax.psum_scatter(holder.reshape(tokens_here * lax.axis_size('seq'), kv_he...]
    psum x1 -> x2, waiting for transfers between devices: 35.1 us -> 40.1 us  [the longest x1 33.7 us: on_device(): lax.psum(weight_part, 'dp')]
  transfers between devices with their start and end apart: 2 -> 3, of which waited for: 1 -> 3; matrix products, arithmetic and copies ran while one was open for 12% -> 11% of each run, Pallas kernels for 0% -> 0%
where the time goes in v1:
time: 200 us; the launch traced here: 199 us
  waiting for transfers between devices  55.3 us (28%)
  matrix products  40.9 us (20%)
  other arithmetic  35.2 us (18%)
  blocking collectives  26.4 us (13%)
  local copies, waits for them, and re-layouts  24.1 us (12%)
  between operations  13.9 us (7%)
  loops' own time  2.88 us (1%)
    psum x1, waiting for transfers between devices, on_device(): lax.psum(weight_part, 'dp')  33.7 us
    scatter-add x1, other arithmetic, on_device(): holder = holder.at[target, :, head_rows, :].add(paired_all, mode='drop')  19 us
    dot_general x4, matrix products, tile_math(): jnp.einsum('ikgd,knjd->kginj', grad_output, value_tile, preferred_element...  16.1 us
    reduce_scatter x1, waiting for transfers between devices, on_device(): lax.psum_scatter(holder.reshape(tokens_here * lax.axis_size('seq'), kv_he...  15.2 us
    all_gather x1, blocking collectives, on_device(): every_logit = lax.all_gather(logit_rows, 'head', axis=1, tiled=True)  13.6 us
    dynamic_slice x16, local copies, waits for them, and re-layouts, on_device(): lax.scan(tile_step, jnp.zeros((), jnp.float32), tile_items)  10.6 us
    dot_general x4, matrix products, tile_math(): jnp.einsum('kginj,ikgd->knjd', prob_low, grad_output, preferred_element_t...  9.55 us
    all_gather x1, blocking collectives, on_device(): lax.all_gather(keys, 'seq', axis=1, tiled=True)  7.12 us
  transfers between devices with their start and end apart: 3, of which 3 were waited for; matrix products, arithmetic and copies ran while one was open for 11% of the time, Pallas kernels for 0%

profile of v1, /device:TPU:0, one launch (start us, length us, event | category | flops | bytes accessed | tf_op | source)
XLA Modules:
  0.0 198.7 jit_solution(16943469141684067259)
XLA Ops:
  8.2 7.1 %all_gather.9 = bf16[1,512,2,128]{3,1,2,0:T(8,128)(2,1)S(1)} all-gather(bf16[1,256,2,128]{3,1,2,0:T(8,128)(2,1)S(1)} %copy.32), channel_id=1, replica_groups=mesh['seq'=2,'head'=4,'dp'=4] {'seq'}, dimensions={1}, use_global_device_ids=true | all-gather | bytes 393216 | tf_op jit(solution)/shard_map/all_gather | solution.py:35
  18.6 5.6 %all_gather.10 = bf16[1,512,2,128]{3,1,2,0:T(8,128)(2,1)S(1)} all-gather(bf16[1,256,2,128]{3,1,2,0:T(8,128)(2,1)S(1)} %copy.35), channel_id=1, replica_groups=mesh['seq'=2,'head'=4,'dp'=4] {'seq'}, dimensions={1}, use_global_device_ids=true | all-gather | bytes 393216 | tf_op jit(solution)/shard_map/all_gather | solution.py:36
  24.2 1.1 gather_fusion
  25.3 2.3 %gather_fusion.1 = bf16[128,64,128]{2,1,0:T(8,128)(2,1)} fusion(bf16[8,64,2,128]{3,1,2,0:T(8,128)(2,1)S(1)} %copy.36, s32[128]{0:T(128)S(1)} %reshape.124), kind=kCustom, calls=%fused_computation.1 | custom fusion | bytes 4195328 | tf_op jit(solution)/shard_map/gather | solution.py:41
  27.7 69.9 %while.16 = (s32[]{:T(128)}, bf16[4,64,2,8,128]{4,3,2,1,0:T(8,128)(2,1)}, bf16[4,64,2,8]{1,3,2,0:T(8,128)(2,1)S(1)}, f32[4,2,16,64,256]{4,3,2,1,0:T(8,128)}, bf1...) while((s32[]{:T(128)}, ...), condition=%wide.region_3.4_spmd.clone.clone, body=%wide.region_0.3_spmd.clone.clone.sunk | while | flops 1355944064 | bytes 33248452 | solution.py:120
  28.7 1.3 fusion.78
  30.0 1.1 constant_dynamic-slice_fusion.11
  34.1 4.0 %fusion.82 = bf16[2,8,64,16,64]{2,4,1,3,0:T(8,128)(2,1)S(1)} fusion(f32[2,16,64,64,8]{3,2,4,1,0:T(8,128)S(1)} %fusion.78, f32[2,8,64]{2,1,0:T(8,128)S(1)} %bitcast.222, f32[2,8,64]{2,1,0:T(8,128)S(1)} %bitcast.223, pred[2,64,16,64]{1,3,2,0:T(8,128)(4,1)S(1)} %compare_and_fusion.2, bf16[4,2,16,64,128]{4,3,2,1,0:T(8,128)(2,1)} %get-tuple-element.380, ...), kind=kOutput, calls=%fused_computation.6.clone.1 | convolution fusion | flops 275120128 | bytes 7221252 | tf_op jit(solution)/shard_map/while/body/eval_jaxpr/ikgd,knjd->kginj/dot_general | solution.py:86
  38.2 1.3 fusion.83
  40.4 2.4 %fusion.85 = f32[2,16,64,128]{3,2,1,0:T(8,128)S(1)} fusion(f32[2,16,64,64,8]{3,2,4,1,0:T(8,128)S(1)} %fusion.78, f32[2,8,64]{2,1,0:T(8,128)S(1)} %bitcast.224, pred[2,64,16,64]{1,3,2,0:T(8,128)(4,1)S(1)} %compare_and_fusion.2, f32[64,2,8]{0,2,1:T(8,128)S(1)} %bitcast.216, bf16[1,64,2,8,128]{4,3,2,1,0:T(8,128)(2,1)S(1)} %get-tuple-element.332), kind=kOutput, calls=%fused_computation.17.clone.1 | convolution fusion | flops 273022976 | bytes 5644288 | tf_op jit(solution)/shard_map/while/body/eval_jaxpr/kginj,ikgd->knjd/dot_general | solution.py:99
  43.7 1.5 fusion.87
  46.2 1.3 fusion.78
  51.6 4.0 %fusion.82 = bf16[2,8,64,16,64]{2,4,1,3,0:T(8,128)(2,1)S(1)} fusion(f32[2,16,64,64,8]{3,2,4,1,0:T(8,128)S(1)} %fusion.78, f32[2,8,64]{2,1,0:T(8,128)S(1)} %bitcast.222, f32[2,8,64]{2,1,0:T(8,128)S(1)} %bitcast.223, pred[2,64,16,64]{1,3,2,0:T(8,128)(4,1)S(1)} %compare_and_fusion.2, bf16[4,2,16,64,128]{4,3,2,1,0:T(8,128)(2,1)} %get-tuple-element.380, ...), kind=kOutput, calls=%fused_computation.6.clone.1 | convolution fusion | flops 275120128 | bytes 7221252 | tf_op jit(solution)/shard_map/while/body/eval_jaxpr/ikgd,knjd->kginj/dot_general | solution.py:86
  55.6 1.3 fusion.83
  57.9 2.4 %fusion.85 = f32[2,16,64,128]{3,2,1,0:T(8,128)S(1)} fusion(f32[2,16,64,64,8]{3,2,4,1,0:T(8,128)S(1)} %fusion.78, f32[2,8,64]{2,1,0:T(8,128)S(1)} %bitcast.224, pred[2,64,16,64]{1,3,2,0:T(8,128)(4,1)S(1)} %compare_and_fusion.2, f32[64,2,8]{0,2,1:T(8,128)S(1)} %bitcast.216, bf16[1,64,2,8,128]{4,3,2,1,0:T(8,128)(2,1)S(1)} %get-tuple-element.332), kind=kOutput, calls=%fused_computation.17.clone.1 | convolution fusion | flops 273022976 | bytes 5644288 | tf_op jit(solution)/shard_map/while/body/eval_jaxpr/kginj,ikgd->knjd/dot_general | solution.py:99
  61.2 1.4 fusion.87
  63.6 1.3 fusion.78
  69.0 4.0 %fusion.82 = bf16[2,8,64,16,64]{2,4,1,3,0:T(8,128)(2,1)S(1)} fusion(f32[2,16,64,64,8]{3,2,4,1,0:T(8,128)S(1)} %fusion.78, f32[2,8,64]{2,1,0:T(8,128)S(1)} %bitcast.222, f32[2,8,64]{2,1,0:T(8,128)S(1)} %bitcast.223, pred[2,64,16,64]{1,3,2,0:T(8,128)(4,1)S(1)} %compare_and_fusion.2, bf16[4,2,16,64,128]{4,3,2,1,0:T(8,128)(2,1)} %get-tuple-element.380, ...), kind=kOutput, calls=%fused_computation.6.clone.1 | convolution fusion | flops 275120128 | bytes 7221252 | tf_op jit(solution)/shard_map/while/body/eval_jaxpr/ikgd,knjd->kginj/dot_general | solution.py:86
  73.1 1.3 fusion.83
  75.3 2.4 %fusion.85 = f32[2,16,64,128]{3,2,1,0:T(8,128)S(1)} fusion(f32[2,16,64,64,8]{3,2,4,1,0:T(8,128)S(1)} %fusion.78, f32[2,8,64]{2,1,0:T(8,128)S(1)} %bitcast.224, pred[2,64,16,64]{1,3,2,0:T(8,128)(4,1)S(1)} %compare_and_fusion.2, f32[64,2,8]{0,2,1:T(8,128)S(1)} %bitcast.216, bf16[1,64,2,8,128]{4,3,2,1,0:T(8,128)(2,1)S(1)} %get-tuple-element.332), kind=kOutput, calls=%fused_computation.17.clone.1 | convolution fusion | flops 273022976 | bytes 5644288 | tf_op jit(solution)/shard_map/while/body/eval_jaxpr/kginj,ikgd->knjd/dot_general | solution.py:99
  78.7 1.5 fusion.87
  81.1 1.3 fusion.78
  86.5 4.0 %fusion.82 = bf16[2,8,64,16,64]{2,4,1,3,0:T(8,128)(2,1)S(1)} fusion(f32[2,16,64,64,8]{3,2,4,1,0:T(8,128)S(1)} %fusion.78, f32[2,8,64]{2,1,0:T(8,128)S(1)} %bitcast.222, f32[2,8,64]{2,1,0:T(8,128)S(1)} %bitcast.223, pred[2,64,16,64]{1,3,2,0:T(8,128)(4,1)S(1)} %compare_and_fusion.2, bf16[4,2,16,64,128]{4,3,2,1,0:T(8,128)(2,1)} %get-tuple-element.380, ...), kind=kOutput, calls=%fused_computation.6.clone.1 | convolution fusion | flops 275120128 | bytes 7221252 | tf_op jit(solution)/shard_map/while/body/eval_jaxpr/ikgd,knjd->kginj/dot_general | solution.py:86
  90.5 1.3 fusion.83
  92.8 2.4 %fusion.85 = f32[2,16,64,128]{3,2,1,0:T(8,128)S(1)} fusion(f32[2,16,64,64,8]{3,2,4,1,0:T(8,128)S(1)} %fusion.78, f32[2,8,64]{2,1,0:T(8,128)S(1)} %bitcast.224, pred[2,64,16,64]{1,3,2,0:T(8,128)(4,1)S(1)} %compare_and_fusion.2, f32[64,2,8]{0,2,1:T(8,128)S(1)} %bitcast.216, bf16[1,64,2,8,128]{4,3,2,1,0:T(8,128)(2,1)S(1)} %get-tuple-element.332), kind=kOutput, calls=%fused_computation.17.clone.1 | convolution fusion | flops 273022976 | bytes 5644288 | tf_op jit(solution)/shard_map/while/body/eval_jaxpr/kginj,ikgd->knjd/dot_general | solution.py:99
  96.1 1.5 fusion.87
  97.7 13.6 %all-gather = bf16[64,256]{1,0:T(8,128)(2,1)S(1)} all-gather(bf16[16,256]{1,0:T(8,128)(2,1)S(1)} %bitcast.227), channel_id=2, replica_groups=mesh['seq'=2,'head'=4,'dp'=4] {'head'}, dimensions={0}, use_global_device_ids=true | all-gather | bytes 40960 | tf_op jit(solution)/shard_map/all_gather | solution.py:138
  112.4 33.7 %all-reduce.3.cloned.1.call-done = f32[64,1280]{1,0:T(8,128)} async-done(((f32[64,1280]{1,0:T(8,128)}), f32[64,1280]{1,0:T(8,128)}) %all-reduce.3.cloned.1.call-update) | async-done | bytes 327696 | tf_op jit(solution)/shard_map/psum | solution.py:141
  146.3 19.0 %scatter_fusion = f32[8,64,2,256]{3,1,2,0:T(8,128)S(1)} fusion(f32[8,64,2,256]{3,1,2,0:T(8,128)S(1)} %broadcast_in_dim.53, s32[128]{0:T(128)S(1)} %reshape.136, f32[128,64,256]{2,1,0:T(8,128)} %bitcast.210), kind=kCustom, calls=%fused_computation.2 | custom fusion | flops 2097152 | bytes 25166848 | tf_op jit(solution)/shard_map/scatter-add | solution.py:127
  166.3 6.4 %all-reduce.5.cloned.1.call-done = f32[64,1280]{1,0:T(8,128)} async-done(((f32[64,1280]{1,0:T(8,128)}), f32[64,1280]{1,0:T(8,128)}) %all-reduce.5.cloned.1.call-update) | async-done | bytes 327696 | tf_op jit(solution)/shard_map/psum | solution.py:141
  172.7 1.7 broadcast_multiply_fusion
  174.4 15.2 %reduce-scatter.2.cloned.1.call-done = bf16[256,2,256]{2,0,1:T(8,128)(2,1)} async-done(((bf16[512,2,256]{2,0,1:T(8,128)(2,1)}), bf16[256,2,256]{2,0,1:T(8,128)(2,1)}) %reduce-scatter.2.cloned.1.call-update) | async-done | bytes 262160 | tf_op jit(solution)/shard_map/reduce_scatter | solution.py:128
  (84 shorter events, 33.1 us)
Async XLA Ops:
  7.2 104.2 %copy-start = (bf16[1,256,1280]{2,1,0:T(8,128)(2,1)S(1)}, bf16[1,256,1280]{2,1,0:T(8,128)(2,1)}, u32[]{:S(2)}) copy-start(bf16[1,256,1280]{2,1,0:T(8,128)(2,1)} %param.19) | copy-start | bytes 1966084
  7.2 20.5 %copy-start.1 = (f32[1,16,256]{2,1,0:T(8,128)S(1)}, f32[1,16,256]{2,1,0:T(8,128)}, u32[]{:S(2)}) copy-start(f32[1,16,256]{2,1,0:T(8,128)} %param.17) | copy-start | bytes 49156
  7.2 138.9 %all-reduce.3.cloned.1.call-start = ((), (), s32[]{:S(2)}) async-start(), calls=%async_computation.2 | async-start | bytes 655360 | tf_op jit(solution)/shard_map/psum | solution.py:141
  112.3 60.4 %all-reduce.5.cloned.1.call-start = ((), (), s32[]{:S(2)}) async-start(), calls=%async_computation.3 | async-start | bytes 655360 | tf_op jit(solution)/shard_map/psum | solution.py:141
  146.1 43.6 %reduce-scatter.2.cloned.1.call-start = ((), (), s32[]{:S(2)}) async-start(), calls=%async_computation.1 | async-start | bytes 786432 | tf_op jit(solution)/shard_map/reduce_scatter | solution.py:128
Sparse Core Ops, SparseCore 0:
  112.4 33.5 all-reduce.2
  148.3 24.3 all-reduce.4
  175.0 14.6 reduce-scatter.1
